TPU v7x, 512 devices: a whole 4x4x16 slice. The times are simulated.
512 devices in a mesh: gx: 4 (over x), gy: 8 (over y, core), gz: 16 (over z).
Axes of the slice: x: 4, y: 4, z: 16, core: 2. Of those that a mesh axis runs over, the one named last changes fastest.
Arguments:
- output_grad: bfloat16 [524288, 1024], P(('gx', 'gy', 'gz')), may hold values from -6 to 6
- entries: int32 [524288, 32], P(('gx', 'gy', 'gz')), may hold values from 0 to 2047, as said below
- weights: bfloat16 [524288, 32], P(('gx', 'gy', 'gz')), may hold values from 0.0099487305 to 0.099609375
- hot_blocks: int32 [512, 16], P(('gx', 'gy', 'gz')), may hold values from -1 to 63, as said below
- block_counts: int32 [512], P(('gx', 'gy', 'gz')), may hold values from 8 to 16, as said below
- param: float32 [4, 16, 128, 1024], P('gx', 'gz', 'gy'), may hold values from -6 to 6
- first_moment: float32 [4, 16, 128, 1024], P('gx', 'gz', 'gy'), may hold values from -4 to 4
- second_moment: float32 [4, 16, 128, 1024], P('gx', 'gz', 'gy'), may hold values from 0.05 to 1
Outputs:
- new_param: float32 [4, 16, 128, 1024], P('gx', 'gz', 'gy')
- new_first: float32 [4, 16, 128, 1024], P('gx', 'gz', 'gy')
- new_second: float32 [4, 16, 128, 1024], P('gx', 'gz', 'gy')
Inputs may be any that keep to these rules, and one draw needn't show every extreme that they name: `hot_blocks`: row d lists device d's hot blocks (block b is rows b * 128 to b * 128 + 127 of the table laid out as 8192 rows) in its first block_counts[d] slots and -1 in the others. The listed blocks of one row differ pairwise modulo 16. Among the devices that differ only in their gz index, some value modulo 16 is listed by every one of them. `block_counts`: among the devices that differ only in their gz index, at least one uses all 16 slots. `entries`: an entry e of a token of device d names a used slot: e // 128 < block_counts[d].
All inputs are finite; a program needn't handle non-finite values.
Results may differ from a plain program's by a relative error of at most 0.00034.
Values sent between devices are 32-bit elements; how exact they have to be, the bound alone decides.
No kernel may reach another device: no remote copies, remote signals or barrier semaphores. Data moves between devices by JAX's collectives and lax.ppermute only.
A program may use at most 128 MiB of HBM per device.

v0:
```python
import jax
import jax.numpy as jnp
from jax import lax
from jax.sharding import PartitionSpec as P

BLOCK = 128


first_decay = 0.9
second_decay = 0.99
learning_rate = 0.01
adam_epsilon = 1e-08
first_debias = 1.0 / (1.0 - 0.9**10)
second_debias = 1.0 / (1.0 - 0.99**10)


def split_up(x, dim, size):
    shape = x.shape
    tiles = x.reshape(*shape[:dim], size, shape[dim] // size, *shape[dim + 1 :])
    return jnp.moveaxis(tiles, dim, 0)


def sum_at_owner(x, axis, dim):
    size = lax.axis_size(axis)
    tiles = lax.all_to_all(split_up(x, dim, size), axis, 0, 0, tiled=True)
    return jnp.sum(tiles, axis=0)


def adam_update(gradient, param, first_moment, second_moment):
    new_first = first_decay * first_moment + (1.0 - first_decay) * gradient
    new_second = second_decay * second_moment + (1.0 - second_decay) * gradient * gradient
    new_param = param - learning_rate * (new_first * first_debias) / (
        jnp.sqrt(new_second * second_debias) + adam_epsilon
    )
    return (new_param, new_first, new_second)


def shards(
    output_grad, entries, weights, hot_blocks, block_counts, param, first_moment, second_moment
):
    line_size = lax.axis_size("gz")
    column_size = lax.axis_size("gx")
    token_count = output_grad.shape[0]
    feature_width = output_grad.shape[1]
    hot_slots = hot_blocks.shape[1]
    listed_blocks = hot_blocks[0]
    slot_index = jnp.arange(hot_slots, dtype=jnp.int32)
    usable = (slot_index < block_counts[0]) & (listed_blocks >= 0)
    safe_blocks = jnp.maximum(listed_blocks, 0)
    slot_bucket = safe_blocks % line_size
    slot_column = safe_blocks // line_size
    entry_slot = entries // BLOCK
    entry_row = entries % BLOCK
    matches = entry_slot[:, :, None] == slot_index
    entry_bucket = jnp.sum(jnp.where(matches, slot_bucket, 0), axis=2)
    entry_kept = jnp.any(matches & usable, axis=2)
    bucket_index = jnp.arange(line_size, dtype=jnp.int32)
    bucket_weighted = jnp.where(
        (entry_bucket[:, :, None] == bucket_index) & entry_kept[:, :, None],
        weights[:, :, None],
        jnp.zeros((), jnp.bfloat16),
    )
    row_index = jnp.arange(BLOCK, dtype=jnp.int32)
    tok_block = 256
    block_total = token_count // tok_block

    def accumulate(step, total):
        start = (step * tok_block).astype(jnp.int32)
        bucket_part = lax.dynamic_slice_in_dim(bucket_weighted, start, tok_block, 0)
        row_part = (
            lax.dynamic_slice_in_dim(entry_row, start, tok_block, 0)[:, :, None] == row_index
        ).astype(jnp.bfloat16)
        grad_part = lax.dynamic_slice_in_dim(output_grad, start, tok_block, 0)
        spread_part = jnp.einsum(
            "tkb,tkr->brt", bucket_part, row_part, preferred_element_type=jnp.float32
        ).astype(jnp.bfloat16)
        return total + jnp.einsum(
            "brt,td->brd", spread_part, grad_part, preferred_element_type=jnp.float32
        )

    partial_value = lax.fori_loop(
        0, block_total, accumulate, jnp.zeros((line_size, BLOCK, feature_width), jnp.float32)
    )
    bucket_hit = (slot_bucket[None, :] == bucket_index[:, None]) & usable[None, :]
    labels = jnp.sum(jnp.where(bucket_hit, slot_column[None, :] + 1, 0), axis=1) - 1
    column_index = jnp.arange(column_size, dtype=jnp.int32)
    received, sources = (
        lax.all_to_all(partial_value, "gz", split_axis=0, concat_axis=0, tiled=True),
        lax.all_to_all(labels.reshape(line_size, 1), "gz", split_axis=0, concat_axis=0, tiled=True),
    )
    selector = (sources[:, 0][None, :] == column_index[:, None]).astype(jnp.float32)
    merged = jnp.einsum(
        "xs,srd->xrd",
        selector,
        received,
        precision=lax.Precision.HIGHEST,
        preferred_element_type=jnp.float32,
    )
    owner_rows = sum_at_owner(merged.reshape(column_size * BLOCK, feature_width), ("gx", "gy"), 0)
    gradient = owner_rows.reshape(param.shape)
    return adam_update(gradient, param, first_moment, second_moment)


def solution(mesh):
    placed = (
        P(("gx", "gy", "gz"), None),
        P(("gx", "gy", "gz"), None),
        P(("gx", "gy", "gz"), None),
        P(("gx", "gy", "gz"), None),
        P(("gx", "gy", "gz")),
        P("gx", "gz", "gy", None),
        P("gx", "gz", "gy", None),
        P("gx", "gz", "gy", None),
    )
    return jax.shard_map(
        shards,
        mesh=mesh,
        in_specs=placed,
        out_specs=(P("gx", "gz", "gy", None), P("gx", "gz", "gy", None), P("gx", "gz", "gy", None)),
        check_vma=False,
    )
```

profile of v0, /device:TPU:1, one launch (start us, length us, event | category | flops | bytes accessed | tf_op | source)
XLA Modules:
  0.0 494.6 jit_solution(2723134939288968572)
XLA Ops:
  1.3 0.7 fusion.26
  1.9 0.7 and_bitcast_fusion
  2.6 0.1 select_reduce_fusion.1
  2.7 0.7 copy.41
  3.4 15.7 %all-to-all-start = ((s32[16,1,1]{2,1,0:T(1,128)}), s32[16,1,1]{2,1,0:T(1,128)S(1)}, u32[]{:S(2)}, u32[]{:S(2)}) async-start(s32[16,1,1]{2,1,0:T(1,128)} %copy.41), calls=%async_computation | async-start | bytes 16384 | tf_op jit(solution)/shard_map/all_to_all | solution.py:89
  19.2 0.7 and_select_fusion
  19.8 0.7 bitcast_and_fusion
  20.5 1.0 copy.49
  21.5 1.1 copy.42
  22.6 0.4 add_select_fusion
  23.1 0.2 copy.46
  23.2 0.6 fusion.17
  23.8 0.5 select_reduce_fusion
  24.4 0.3 copy.48
  24.6 0.2 copy.47
  24.8 4.2 fusion.15
  29.1 43.0 %while.14 = (s32[]{:T(128)}, f32[16,128,1024]{2,1,0:T(8,128)}, s32[1024,32]{1,0:T(8,128)S(1)}, bf16[1024,32,16]{1,2,0:T(8,128)(2,1)}, bf16[1024,1024]{1,0:T(8,12...) while((s32[]{:T(128)}, f32[16,128,1024]{2,1,0:T(8,128)}, s32[1024,32]{1,0:T(8,128)S(1)}, ...), condition=%wide.region_4.5_spmd.clone, body=%wide.region_3.4_spmd.clone.sunk | while | flops 1113063424 | bytes 20545704 | solution.py:81
  29.1 3.1 fusion.36
  32.2 5.7 %select_add_fusion.2 = f32[16,128,1024]{2,1,0:T(8,128)} fusion(f32[16,128,1024]{2,1,0:T(8,128)} %get-tuple-element.191, pred[]{:T(512)S(6)} %compare.12, bf16[16,128,256]{1,0,2:T(8,128)(2,1)S(1)} %fusion.36, bf16[1024,1024]{1,0:T(8,128)(2,1)} %get-tuple-element.203, s32[]{:T(128)S(6)} %select_n.70), kind=kOutput, calls=%fused_computation.1.clone.1 | convolution fusion | flops 1077936128 | bytes 18350084 | tf_op jit(solution)/shard_map/while/body/eval_jaxpr/brt,td->brd/dot_general | solution.py:77
  37.9 3.1 fusion.36
  41.1 8.2 %select_add_fusion.2 = f32[16,128,1024]{2,1,0:T(8,128)} fusion(f32[16,128,1024]{2,1,0:T(8,128)} %get-tuple-element.191, pred[]{:T(512)S(6)} %compare.12, bf16[16,128,256]{1,0,2:T(8,128)(2,1)S(1)} %fusion.36, bf16[1024,1024]{1,0:T(8,128)(2,1)} %get-tuple-element.203, s32[]{:T(128)S(6)} %select_n.70), kind=kOutput, calls=%fused_computation.1.clone.1 | convolution fusion | flops 1077936128 | bytes 18350084 | tf_op jit(solution)/shard_map/while/body/eval_jaxpr/brt,td->brd/dot_general | solution.py:77
  49.3 3.1 fusion.36
  52.4 8.3 %select_add_fusion.2 = f32[16,128,1024]{2,1,0:T(8,128)} fusion(f32[16,128,1024]{2,1,0:T(8,128)} %get-tuple-element.191, pred[]{:T(512)S(6)} %compare.12, bf16[16,128,256]{1,0,2:T(8,128)(2,1)S(1)} %fusion.36, bf16[1024,1024]{1,0:T(8,128)(2,1)} %get-tuple-element.203, s32[]{:T(128)S(6)} %select_n.70), kind=kOutput, calls=%fused_computation.1.clone.1 | convolution fusion | flops 1077936128 | bytes 18350084 | tf_op jit(solution)/shard_map/while/body/eval_jaxpr/brt,td->brd/dot_general | solution.py:77
  60.7 3.1 fusion.36
  63.8 8.3 %select_add_fusion.2 = f32[16,128,1024]{2,1,0:T(8,128)} fusion(f32[16,128,1024]{2,1,0:T(8,128)} %get-tuple-element.191, pred[]{:T(512)S(6)} %compare.12, bf16[16,128,256]{1,0,2:T(8,128)(2,1)S(1)} %fusion.36, bf16[1024,1024]{1,0:T(8,128)(2,1)} %get-tuple-element.203, s32[]{:T(128)S(6)} %select_n.70), kind=kOutput, calls=%fused_computation.1.clone.1 | convolution fusion | flops 1077936128 | bytes 18350084 | tf_op jit(solution)/shard_map/while/body/eval_jaxpr/brt,td->brd/dot_general | solution.py:77
  72.1 0.0 all-to-all-done
  72.1 11.5 %all-to-all-start.1 = ((f32[16,128,1024]{2,1,0:T(8,128)}), f32[16,128,1024]{2,1,0:T(8,128)}, u32[]{:S(2)}, u32[]{:S(2)}) async-start(f32[16,128,1024]{2,1,0:T(8,128)} %get-tuple-element.112), calls=%async_computation.1 | async-start | bytes 16777216 | tf_op jit(solution)/shard_map/all_to_all | solution.py:88
  83.6 0.4 reduce
  84.0 361.2 %all-to-all-done.1 = f32[16,128,1024]{2,1,0:T(8,128)} async-done(((f32[16,128,1024]{2,1,0:T(8,128)}), f32[16,128,1024]{2,1,0:T(8,128)}, u32[]{:S(2)}, u32[]{:S(2)}) %all-to-all-start.1) | async-done | bytes 8388640 | tf_op jit(solution)/shard_map/all_to_all | solution.py:88
  445.2 10.7 %fusion.12 = f32[4,128,1024]{2,0,1:T(4,128)S(1)} fusion(f32[16,128,1024]{2,1,0:T(8,128)} %all-to-all-done.1, s32[16]{0:T(128)S(1)} %reduce), kind=kOutput, calls=%fused_computation.14 | convolution fusion | flops 100663360 | bytes 10485824 | tf_op jit(solution)/shard_map/xs,srd->xrd/dot_general | solution.py:92
  455.9 1.2 copy.51
  457.2 0.0 copy-start
  457.2 0.0 copy-start.1
  457.2 0.0 copy-start.2
  457.2 36.6 %all_to_all.16 = f32[32,16,1024]{2,1,0:T(8,128)S(1)} all-to-all(f32[32,16,1024]{2,1,0:T(8,128)S(1)} %bitcast.35), channel_id=1, replica_groups=mesh['gx'=4,'gy'=8,'gz'=16] {'gx','gy'}, dimensions={0} | all-to-all | bytes 4194304 | tf_op jit(solution)/shard_map/all_to_all | solution.py:25
  493.8 0.1 reduce_sum.31
  493.9 0.0 copy-done
  493.9 0.0 copy-done.1
  493.9 0.0 copy-done.2
  493.9 0.7 divide_subtract_fusion
  (6 shorter events, 0.0 us)
Async XLA Ops:
  3.4 68.7 %all-to-all-start = ((s32[16,1,1]{2,1,0:T(1,128)}), s32[16,1,1]{2,1,0:T(1,128)S(1)}, u32[]{:S(2)}, u32[]{:S(2)}) async-start(s32[16,1,1]{2,1,0:T(1,128)} %copy.41), calls=%async_computation | async-start | bytes 16384 | tf_op jit(solution)/shard_map/all_to_all | solution.py:89
  72.1 373.1 %all-to-all-start.1 = ((f32[16,128,1024]{2,1,0:T(8,128)}), f32[16,128,1024]{2,1,0:T(8,128)}, u32[]{:S(2)}, u32[]{:S(2)}) async-start(f32[16,128,1024]{2,1,0:T(8,128)} %get-tuple-element.112), calls=%async_computation.1 | async-start | bytes 16777216 | tf_op jit(solution)/shard_map/all_to_all | solution.py:88
  457.2 36.7 %copy-start = (f32[1,1,16,1024]{3,2,1,0:T(8,128)S(1)}, f32[1,1,16,1024]{3,2,1,0:T(8,128)}, u32[]{:S(2)}) copy-start(f32[1,1,16,1024]{3,2,1,0:T(8,128)} %param.15) | copy-start | bytes 196612
  457.2 36.7 %copy-start.1 = (f32[1,1,16,1024]{3,2,1,0:T(8,128)S(1)}, f32[1,1,16,1024]{3,2,1,0:T(8,128)}, u32[]{:S(2)}) copy-start(f32[1,1,16,1024]{3,2,1,0:T(8,128)} %param.16) | copy-start | bytes 196612
  457.2 36.7 %copy-start.2 = (f32[1,1,16,1024]{3,2,1,0:T(8,128)S(1)}, f32[1,1,16,1024]{3,2,1,0:T(8,128)}, u32[]{:S(2)}) copy-start(f32[1,1,16,1024]{3,2,1,0:T(8,128)} %param.17) | copy-start | bytes 196612
where the time goes:
time: 495 us
  waiting for transfers between devices  361 us (73%)
  matrix products  53.6 us (11%)
  blocking collectives  36.6 us (7%)
  starting transfers between devices  27.3 us (6%)
  other arithmetic  9.78 us (2%)
    all_to_all x1, waiting for transfers between devices, shards(): lax.all_to_all(partial_value, 'gz', split_axis=0, concat_axis=0, tiled=True)  361 us
    all_to_all x1, blocking collectives, sum_at_owner(): tiles = lax.all_to_all(split_up(x, dim, size), axis, 0, 0, tiled=True)  36.6 us
    dot_general x4, matrix products, accumulate(): jnp.einsum('brt,td->brd', spread_part, grad_part, preferred_element_type=...  30.5 us
    all_to_all x1, starting transfers between devices, shards(): lax.all_to_all(labels.reshape(line_size, 1), 'gz', split_axis=0, concat_a...  15.7 us
    dot_general x4, matrix products, accumulate(): jnp.einsum('tkb,tkr->brt', bucket_part, row_part, preferred_element_type=...  12.4 us
    all_to_all x1, starting transfers between devices, shards(): lax.all_to_all(partial_value, 'gz', split_axis=0, concat_axis=0, tiled=True)  11.5 us
    dot_general x1, matrix products, shards(): jnp.einsum('xs,srd->xrd', selector, received, precision=lax.Precision.HIG...  10.7 us
  transfers between devices with their start and end apart: 2, of which 1 were waited for; matrix products, arithmetic and copies ran while one was open for 11% of the time, Pallas kernels for 0%

commit v1 on v0

v1 whole, which is shorter than its diff:
```python
import jax
import jax.numpy as jnp
from jax import lax
from jax.experimental import pallas as pl
from jax.experimental.pallas import tpu as pltpu
from jax.sharding import PartitionSpec as P

BLOCK = 128
F32 = jnp.float32
BF16 = jnp.bfloat16

first_decay = 0.9
second_decay = 0.99
learning_rate = 0.01
adam_epsilon = 1e-08
first_debias = 1.0 / (1.0 - 0.9**10)
second_debias = 1.0 / (1.0 - 0.99**10)


def spread_body(ent_ref, wgt_ref, out_ref):
    groups = ent_ref.shape[1]
    sub = lax.broadcasted_iota(jnp.int32, (128, 256), 0)
    tok = lax.broadcasted_iota(jnp.int32, (1, 256), 1) // 32

    def pair(p, carry):
        halves = []
        for h in range(2):
            ent = ent_ref[0, pl.ds(2 * p + h, 1), :]
            wgt = wgt_ref[0, pl.ds(2 * p + h, 1), :]
            row = ent & (BLOCK - 1)
            key = (ent >> 7) * 8 + tok
            rows = jnp.where(sub == row, 1.0, 0.0).astype(BF16)
            keys = jnp.where(sub == key, wgt, 0.0).astype(BF16)
            one = lax.dot_general(
                keys, rows, (((1,), (1,)), ((), ())), preferred_element_type=F32
            )
            halves.append(one.reshape(16, 8, BLOCK))
        both = jnp.concatenate(halves, axis=1).astype(BF16)
        start = pl.multiple_of(p * 16, 16)
        for b in range(16):
            out_ref[0, pl.ds(start, 16), b * BLOCK : (b + 1) * BLOCK] = both[b]
        return carry

    lax.fori_loop(0, groups // 2, pair, 0, unroll=4)


def spread_of(entries, weights):
    sources, groups, lanes = entries.shape
    step = 32
    return pl.pallas_call(
        spread_body,
        grid=(sources, groups // step),
        in_specs=[
            pl.BlockSpec((1, step, lanes), lambda s, i: (s, i, 0)),
            pl.BlockSpec((1, step, lanes), lambda s, i: (s, i, 0)),
        ],
        out_specs=pl.BlockSpec((1, step * 8, 2048), lambda s, i: (s, i, 0)),
        out_shape=jax.ShapeDtypeStruct((sources, groups * 8, 2048), BF16),
        cost_estimate=pl.CostEstimate(
            flops=sources * groups * 2 * 128 * 256 * 128 * 4,
            bytes_accessed=sources * groups * 8 * 4096,
            transcendentals=0,
        ),
        name="spread",
    )(entries, weights)


def merge_body(col_ref, grad_ref, spread_ref, own_ref, send_ref):
    s = pl.program_id(0)

    @pl.when(s == 0)
    def _():
        own_ref[...] = jnp.zeros_like(own_ref)
        send_ref[...] = jnp.zeros_like(send_ref)

    grad = grad_ref[0].astype(BF16)

    def pair(p, carry):
        start = pl.multiple_of(p * 256, 256)
        part = lax.dot_general(
            spread_ref[0, :, pl.ds(start, 256)],
            grad,
            (((0,), (0,)), ((), ())),
            preferred_element_type=F32,
        )
        for h in range(2):
            bucket = 2 * p + h
            place = (bucket & 3) * 4 + (bucket >> 2)
            col = col_ref[s, bucket]
            for y in range(4):
                at = h * 128 + y * 32
                own_ref[y, place, col] += part[at : at + 16]
                send_ref[y, place, col] += part[at + 16 : at + 32]
        return carry

    lax.fori_loop(0, 8, pair, 0)


def merge(cols, grads, spreads):
    sources, tokens, width = grads.shape
    dense = jax.ShapeDtypeStruct((4, 16, 4, 16, width), F32)
    block = pl.BlockSpec((4, 16, 4, 16, width), lambda s, c: (0, 0, 0, 0, 0))
    return pl.pallas_call(
        merge_body,
        grid_spec=pltpu.PrefetchScalarGridSpec(
            num_scalar_prefetch=1,
            grid=(sources,),
            in_specs=[
                pl.BlockSpec((1, tokens, width), lambda s, c: (s, 0, 0)),
                pl.BlockSpec((1, tokens, 2048), lambda s, c: (s, 0, 0)),
            ],
            out_specs=[block, block],
        ),
        out_shape=[dense, dense],
        cost_estimate=pl.CostEstimate(
            flops=sources * 2 * 2048 * tokens * width,
            bytes_accessed=sources * tokens * (4096 + 4 * width) + 2**23,
            transcendentals=0,
        ),
        name="merge",
    )(cols, grads, spreads)


def adam_update(gradient, param, first_moment, second_moment):
    new_first = first_decay * first_moment + (1.0 - first_decay) * gradient
    new_second = second_decay * second_moment + (1.0 - second_decay) * gradient * gradient
    new_param = param - learning_rate * (new_first * first_debias) / (
        jnp.sqrt(new_second * second_debias) + adam_epsilon
    )
    return (new_param, new_first, new_second)


def shards(
    output_grad, entries, weights, hot_blocks, block_counts, param, first_moment, second_moment
):
    tokens, width = output_grad.shape
    core = lax.axis_index("gy") % 2
    listed = hot_blocks[0]
    slots = jnp.arange(16, dtype=jnp.int32)
    usable = (slots < block_counts[0]) & (listed >= 0)
    safe = jnp.maximum(listed, 0)
    slot_bucket = safe % 16
    hit = (slot_bucket[None, :] == slots[:, None]) & usable[None, :]
    cols = jnp.sum(jnp.where(hit, (safe // 16)[None, :], 0), axis=1)

    match = (entries >> 7)[:, :, None] == slots
    bucket = jnp.sum(jnp.where(match, slot_bucket, 0), axis=2)
    kept = jnp.any(match & usable, axis=2)
    code = bucket * BLOCK + ((entries & (BLOCK - 1)) ^ (core * 16))
    kept_weights = jnp.where(kept, weights.astype(F32), 0.0)
    small = jnp.concatenate(
        [
            code.astype(F32).reshape(128, 256),
            kept_weights.reshape(128, 256),
            jnp.broadcast_to(jnp.pad(cols.astype(F32), (0, 240))[None], (8, 256)),
        ],
        axis=0,
    )
    small = lax.all_to_all(jnp.broadcast_to(small[None], (4, 264, 256)), "gx", 0, 0, tiled=True)
    wide = jnp.swapaxes(output_grad.astype(F32).reshape(tokens, 4, width // 4), 0, 1)
    grads = lax.all_to_all(wide, "gx", 0, 0, tiled=True)

    spreads = spread_of(small[:, :128].astype(jnp.int32), small[:, 128:256])
    col_table = small[:, 256, :16].astype(jnp.int32)
    own, send = merge(col_table, grads, spreads)
    got = lax.ppermute(send, "gy", [(i, i ^ 1) for i in range(8)])
    chip = own + got
    rows = lax.all_to_all(
        chip, "gy", 0, 0, axis_index_groups=[[0, 2, 4, 6], [1, 3, 5, 7]], tiled=True
    )
    rows = jnp.sum(rows, axis=0)
    near = lax.all_to_all(
        rows.reshape(4, 4, 4, 16, width // 4),
        "gz",
        0,
        0,
        axis_index_groups=[[4 * h + i for i in range(4)] for h in range(4)],
        tiled=True,
    )
    near = jnp.sum(near, axis=0)
    far = lax.all_to_all(
        near.reshape(16, 16, width // 4),
        ("gx", "gz"),
        0,
        0,
        axis_index_groups=[
            [x * 16 + 4 * h + i for h in range(4) for x in range(4)] for i in range(4)
        ],
        tiled=True,
    )
    far = jnp.sum(far.reshape(4, 4, 16, width // 4), axis=0)
    gradient = jnp.swapaxes(far, 0, 1).reshape(param.shape)
    return adam_update(gradient, param, first_moment, second_moment)


def solution(mesh):
    placed = (
        P(("gx", "gy", "gz"), None),
        P(("gx", "gy", "gz"), None),
        P(("gx", "gy", "gz"), None),
        P(("gx", "gy", "gz"), None),
        P(("gx", "gy", "gz")),
        P("gx", "gz", "gy", None),
        P("gx", "gz", "gy", None),
        P("gx", "gz", "gy", None),
    )
    return jax.shard_map(
        shards,
        mesh=mesh,
        in_specs=placed,
        out_specs=(P("gx", "gz", "gy", None), P("gx", "gz", "gy", None), P("gx", "gz", "gy", None)),
        check_vma=False,
    )
```

time: 495 us -> 234 us (0.47)
  waiting for transfers between devices: 361 us -> 28.6 us
  blocking collectives: 36.6 us -> 117 us
  matrix products: 53.6 us -> 0 us
  Pallas kernels: 0 us -> 42.9 us
  starting transfers between devices: 27.3 us -> 19.1 us
    all_to_all x2, waiting for transfers between devices: 361 us -> 21.7 us  [the longest x1 17.6 us: shards(): grads = lax.all_to_all(wide, 'gx', 0, 0, tiled=True)]
    all_to_all x1 -> x3, blocking collectives: 36.6 us -> 117 us  [the longest x1 56.7 us: shards(): lax.all_to_all(chip, 'gy', 0, 0, axis_index_groups=[[0, 2, 4, 6], [1, 3,...]
    dot_general x9 -> x0, matrix products: 53.6 us -> none  [the longest x4 30.5 us: accumulate(): jnp.einsum('brt,td->brd', spread_part, grad_part, preferred_element_type=...]
    pallas_call x0 -> x2, Pallas kernels: none -> 42.9 us  [the longest x1 23 us: spread_of(): pl.pallas_call(spread_body, grid=(sources, groups // step), in_specs=[pl....]
    all_to_all x2, starting transfers between devices: 27.3 us -> 9.69 us  [the longest x1 4.86 us: shards(): grads = lax.all_to_all(wide, 'gx', 0, 0, tiled=True)]
    ppermute x0 -> x1, starting transfers between devices: none -> 9.37 us  [shards(): got = lax.ppermute(send, 'gy', [(i, i ^ 1) for i in range(8)])]
    ppermute x0 -> x1, waiting for transfers between devices: none -> 6.97 us  [shards(): got = lax.ppermute(send, 'gy', [(i, i ^ 1) for i in range(8)])]
  transfers between devices with their start and end apart: 2 -> 3, of which waited for: 1 -> 3; matrix products, arithmetic and copies ran while one was open for 11% -> 3% of each run, Pallas kernels for 0% -> 10%
where the time goes in v1:
time: 234 us; the launch traced here: 232 us
  blocking collectives  117 us (50%)
  Pallas kernels  42.9 us (18%)
  waiting for transfers between devices  28.6 us (12%)
  starting transfers between devices  19.1 us (8%)
  other arithmetic  14.3 us (6%)
  local copies, waits for them, and re-layouts  7.82 us (3%)
    all_to_all x1, blocking collectives, shards(): lax.all_to_all(chip, 'gy', 0, 0, axis_index_groups=[[0, 2, 4, 6], [1, 3,...  56.7 us
    all_to_all x1, blocking collectives, shards(): lax.all_to_all(rows.reshape(4, 4, 4, 16, width // 4), 'gz', 0, 0, axis_in...  30.3 us
    all_to_all x1, blocking collectives, shards(): lax.all_to_all(near.reshape(16, 16, width // 4), ('gx', 'gz'), 0, 0, axis...  30.2 us
    pallas_call x1, Pallas kernels, spread_of(): pl.pallas_call(spread_body, grid=(sources, groups // step), in_specs=[pl....  23 us
    pallas_call x1, Pallas kernels, merge(): pl.pallas_call(merge_body, grid_spec=pltpu.PrefetchScalarGridSpec(num_sca...  20 us
    all_to_all x1, waiting for transfers between devices, shards(): grads = lax.all_to_all(wide, 'gx', 0, 0, tiled=True)  17.6 us
    ppermute x1, starting transfers between devices, shards(): got = lax.ppermute(send, 'gy', [(i, i ^ 1) for i in range(8)])  9.37 us
    ppermute x1, waiting for transfers between devices, shards(): got = lax.ppermute(send, 'gy', [(i, i ^ 1) for i in range(8)])  6.97 us
  transfers between devices with their start and end apart: 3, of which 3 were waited for; matrix products, arithmetic and copies ran while one was open for 3% of the time, Pallas kernels for 10%

profile of v1, /device:TPU:1, one launch (start us, length us, event | category | flops | bytes accessed | tf_op | source)
XLA Modules:
  0.0 231.5 jit_solution(16228425629092164621)
XLA Ops:
  0.6 0.0 copy-start
  0.6 0.7 and_select_fusion.2
  1.3 0.7 fusion.4
  2.7 0.7 and_bitcast_fusion
  3.3 0.7 bitcast_and_fusion
  4.0 0.1 select_reduce_fusion.1
  4.1 0.9 broadcast_shift-right-arithmetic_fusion
  5.0 0.6 fusion.1
  5.6 0.5 select_reduce_fusion
  6.2 0.9 convert_select_fusion
  7.0 0.2 copy.22
  7.2 0.2 reshape.92
  7.4 0.0 copy-done
  7.5 0.2 copy.21
  7.7 0.2 reshape.91
  7.9 1.1 broadcast_in_dim.52
  9.0 4.8 %all-to-all-start = ((f32[4,264,256]{2,1,0:T(8,128)}), f32[4,264,256]{2,1,0:T(8,128)S(1)}, u32[]{:S(2)}, u32[]{:S(2)}) async-start(f32[4,264,256]{2,1,0:T(8,128)} %broadcast_in_dim.52), calls=%async_computation | async-start | bytes 2162688 | tf_op jit(solution)/shard_map/all_to_all | solution.py:159
  13.8 2.9 %copy.23 = bf16[1024,1024]{0,1:T(8,128)(2,1)S(1)} copy(bf16[1024,1024]{1,0:T(8,128)(2,1)} %param.8) | data formatting | bytes 4194304 | tf_op args[0]
  16.7 3.0 %copy.24 = f32[1024,4,256]{2,0,1:T(8,128)} copy(bf16[1024,4,256]{0,2,1:T(8,128)(2,1)S(1)} %bitcast.22) | data formatting | bytes 6291456 | tf_op jit(solution)/shard_map/transpose | solution.py:160
  19.7 4.0 %all-to-all-done = f32[4,264,256]{2,1,0:T(8,128)S(1)} async-done(((f32[4,264,256]{2,1,0:T(8,128)}), f32[4,264,256]{2,1,0:T(8,128)S(1)}, u32[]{:S(2)}, u32[]{:S(2)}) %all-to-all-start) | async-done | bytes 1081376 | tf_op jit(solution)/shard_map/all_to_all | solution.py:159
  23.7 4.9 %all-to-all-start.1 = ((f32[4,1024,256]{2,1,0:T(8,128)}), f32[4,1024,256]{2,1,0:T(8,128)}, u32[]{:S(2)}, u32[]{:S(2)}) async-start(f32[4,1024,256]{2,1,0:T(8,128)} %bitcast.21), calls=%async_computation.1 | async-start | bytes 8388608 | tf_op jit(solution)/shard_map/all_to_all | solution.py:161
  28.6 0.6 slice_convert_fusion.1
  29.2 1.2 fusion.7
  30.4 23.0 %spread.1.spread_ref = bf16[4,1024,2048]{2,1,0:T(8,128)(2,1)} custom-call(s32[4,128,256]{2,1,0:T(8,128)} %get-tuple-element.11.ent_ref, f32[4,128,256]{2,1,0:T(8,128)} %get-tuple-element.10.wgt_ref), custom_call_target="tpu_custom_call" | custom-call | flops 17179869184 | bytes 16777216 | tf_op jit(solution)/shard_map/spread/pallas_call | solution.py:50
  53.3 17.6 %all-to-all-done.1.grad_ref = f32[4,1024,256]{2,1,0:T(8,128)} async-done(((f32[4,1024,256]{2,1,0:T(8,128)}), f32[4,1024,256]{2,1,0:T(8,128)}, u32[]{:S(2)}, u32[]{:S(2)}) %all-to-all-start.1) | async-done | bytes 4194336 | tf_op jit(solution)/shard_map/all_to_all | solution.py:161
  70.9 20.0 %merge.1 = (f32[4,16,4,16,256]{4,3,2,1,0:T(8,128)}, f32[4,16,4,16,256]{4,3,2,1,0:T(8,128)}) custom-call(s32[4,16]{1,0:T(4,128)} %bitcast.27, f32[4,1024,256]{2,1,0:T(8,128)} %all-to-all-done.1.grad_ref, bf16[4,1024,2048]{2,1,0:T(8,128)(2,1)} %spread.1.spread_ref), custom_call_target="tpu_custom_call" | custom-call | flops 4294967296 | bytes 29360128 | tf_op jit(solution)/shard_map/merge/pallas_call | solution.py:103
  90.9 9.4 %collective-permute-start = (f32[4,16,4,16,256]{4,3,2,1,0:T(8,128)}, f32[4,16,4,16,256]{4,3,2,1,0:T(8,128)S(1)}, u32[]{:S(2)}, u32[]{:S(2)}) collective-permute-start(f32[4,16,4,16,256]{4,3,2,1,0:T(8,128)} %get-tuple-element.6), channel_id=1, source_target_pairs={{0,16},{16,0},{32,48},{48,32},{64,80},{80,64},{96,112},{112,96},{1... | collective-permute-start | bytes 12582920 | tf_op jit(solution)/shard_map/ppermute | solution.py:166
  100.3 7.0 %collective-permute-done = f32[4,16,4,16,256]{4,3,2,1,0:T(8,128)S(1)} collective-permute-done((f32[4,16,4,16,256]{4,3,2,1,0:T(8,128)}, f32[4,16,4,16,256]{4,3,2,1,0:T(8,128)S(1)}, u32[]{:S(2)}, u32[]{:S(2)}) %collective-permute-start) | collective-permute-done | bytes 4194336 | tf_op jit(solution)/shard_map/ppermute | solution.py:166
  107.3 3.2 %add.39 = f32[4,16,4,16,256]{4,3,2,1,0:T(8,128)S(1)} add(f32[4,16,4,16,256]{4,3,2,1,0:T(8,128)} %get-tuple-element.5, f32[4,16,4,16,256]{4,3,2,1,0:T(8,128)S(1)} %collective-permute-done) | non-fusion elementwise | flops 1048576 | bytes 12582912 | tf_op jit(solution)/shard_map/add | solution.py:167
  110.5 56.7 %all_to_all.25 = f32[4,16,4,16,256]{4,3,2,1,0:T(8,128)} all-to-all(f32[4,16,4,16,256]{4,3,2,1,0:T(8,128)S(1)} %add.39), channel_id=1, replica_groups={{0,32,64,96},{16,48,80,112},{1,33,65,97},{17,49,81,113},{2,34,66,98},{1..., dimensions={0} | all-to-all | bytes 8388608 | tf_op jit(solution)/shard_map/all_to_all | solution.py:168
  167.2 2.8 %reduce_sum.47 = f32[16,4,16,256]{3,2,1,0:T(8,128)S(1)} reduce(f32[4,16,4,16,256]{4,3,2,1,0:T(8,128)} %all_to_all.25, f32[]{:T(128)} %constant.70.clone.1), dimensions={0}, to_apply=%region_3.4 | reduce | flops 786432 | bytes 5242884 | tf_op jit(solution)/shard_map/reduce_sum | solution.py:171
  170.0 0.0 copy-start.1
  170.0 0.0 copy-start.2
  170.0 0.0 copy-start.3
  170.0 30.3 %all_to_all.26 = f32[4,4,4,16,256]{4,3,2,1,0:T(8,128)S(1)} all-to-all(f32[4,4,4,16,256]{4,3,2,1,0:T(8,128)S(1)} %bitcast.23), channel_id=1, replica_groups={{0,1,2,3},{4,5,6,7},{8,9,10,11},{12,13,14,15},{16,17,18,19},{20,21,22,2..., dimensions={0} | all-to-all | bytes 2097152 | tf_op jit(solution)/shard_map/all_to_all | solution.py:172
  200.4 0.1 reduce_sum.48
  200.5 30.2 %all_to_all.27 = f32[16,16,256]{2,1,0:T(8,128)S(1)} all-to-all(f32[16,16,256]{2,1,0:T(8,128)S(1)} %bitcast.24), channel_id=1, replica_groups={{0,128,256,384,4,132,260,388,8,136,264,392,12,140,268,396},{1,129,257,3..., dimensions={0} | all-to-all | bytes 524288 | tf_op jit(solution)/shard_map/all_to_all | solution.py:181
  230.8 0.0 copy-done.1
  230.8 0.0 copy-done.2
  230.8 0.0 copy-done.3
  230.8 0.7 divide_subtract_fusion
  (8 shorter events, 0.2 us)
Async XLA Ops:
  0.6 6.8 %copy-start = (s32[1024,32]{0,1:T(8,128)S(1)}, s32[1024,32]{0,1:T(8,128)}, u32[]{:S(2)}) copy-start(s32[1024,32]{0,1:T(8,128)} %param.9) | copy-start | bytes 393220
  9.0 14.8 %all-to-all-start = ((f32[4,264,256]{2,1,0:T(8,128)}), f32[4,264,256]{2,1,0:T(8,128)S(1)}, u32[]{:S(2)}, u32[]{:S(2)}) async-start(f32[4,264,256]{2,1,0:T(8,128)} %broadcast_in_dim.52), calls=%async_computation | async-start | bytes 2162688 | tf_op jit(solution)/shard_map/all_to_all | solution.py:159
  23.7 47.2 %all-to-all-start.1 = ((f32[4,1024,256]{2,1,0:T(8,128)}), f32[4,1024,256]{2,1,0:T(8,128)}, u32[]{:S(2)}, u32[]{:S(2)}) async-start(f32[4,1024,256]{2,1,0:T(8,128)} %bitcast.21), calls=%async_computation.1 | async-start | bytes 8388608 | tf_op jit(solution)/shard_map/all_to_all | solution.py:161
  90.9 16.4 %collective-permute-start = (f32[4,16,4,16,256]{4,3,2,1,0:T(8,128)}, f32[4,16,4,16,256]{4,3,2,1,0:T(8,128)S(1)}, u32[]{:S(2)}, u32[]{:S(2)}) collective-permute-start(f32[4,16,4,16,256]{4,3,2,1,0:T(8,128)} %get-tuple-element.6), channel_id=1, source_target_pairs={{0,16},{16,0},{32,48},{48,32},{64,80},{80,64},{96,112},{112,96},{1... | collective-permute-start | bytes 12582920 | tf_op jit(solution)/shard_map/ppermute | solution.py:166
  170.0 60.8 %copy-start.1 = (f32[1,1,16,1024]{3,2,1,0:T(8,128)S(1)}, f32[1,1,16,1024]{3,2,1,0:T(8,128)}, u32[]{:S(2)}) copy-start(f32[1,1,16,1024]{3,2,1,0:T(8,128)} %param.13) | copy-start | bytes 196612
  170.0 60.8 %copy-start.2 = (f32[1,1,16,1024]{3,2,1,0:T(8,128)S(1)}, f32[1,1,16,1024]{3,2,1,0:T(8,128)}, u32[]{:S(2)}) copy-start(f32[1,1,16,1024]{3,2,1,0:T(8,128)} %param.14) | copy-start | bytes 196612
  170.0 60.8 %copy-start.3 = (f32[1,1,16,1024]{3,2,1,0:T(8,128)S(1)}, f32[1,1,16,1024]{3,2,1,0:T(8,128)}, u32[]{:S(2)}) copy-start(f32[1,1,16,1024]{3,2,1,0:T(8,128)} %param.15) | copy-start | bytes 196612

commit v2 on v1

v2 whole, which is shorter than its diff:
```python
import jax
import jax.numpy as jnp
from jax import lax
from jax.experimental import pallas as pl
from jax.experimental.pallas import tpu as pltpu
from jax.sharding import PartitionSpec as P


BLOCK = 128
F32 = jnp.float32
BF16 = jnp.bfloat16

first_decay = 0.9
second_decay = 0.99
learning_rate = 0.01
adam_epsilon = 1e-08
first_debias = 1.0 / (1.0 - 0.9**10)
second_debias = 1.0 / (1.0 - 0.99**10)


def widen_body(grad_ref, first_ref, second_ref):
    wide = grad_ref[...].astype(F32)
    first_ref[0] = wide[:, :128]
    second_ref[0] = wide[:, 128:]


def widen(grads):
    tokens, width = grads.shape
    chunk = jax.ShapeDtypeStruct((4, tokens, width // 8), F32)
    spec = pl.BlockSpec((1, tokens, width // 8), lambda x: (x, 0, 0))
    return pl.pallas_call(
        widen_body,
        grid=(4,),
        in_specs=[pl.BlockSpec((tokens, width // 4), lambda x: (0, x))],
        out_specs=[spec, spec],
        out_shape=[chunk, chunk],
        cost_estimate=pl.CostEstimate(flops=2**23, bytes_accessed=6 * 2**20, transcendentals=0),
        name="widen",
    )(grads)


def spread_body(code_ref, wgt_ref, out_ref, turned_ref):
    sub = lax.broadcasted_iota(jnp.int32, (128, 256), 0)
    tok = lax.broadcasted_iota(jnp.int32, (1, 256), 1) // 32

    def pair(p, carry):
        halves = []
        for h in range(2):
            code = code_ref[0, pl.ds(2 * p + h, 1), :].astype(jnp.int32)
            wgt = wgt_ref[0, pl.ds(2 * p + h, 1), :]
            row = code & (BLOCK - 1)
            key = (code >> 7) * 8 + tok
            rows = jnp.where(sub == row, 1.0, 0.0).astype(BF16)
            keys = jnp.where(sub == key, wgt, 0.0).astype(BF16)
            one = lax.dot_general(
                keys, rows, (((1,), (1,)), ((), ())), preferred_element_type=F32
            )
            halves.append(one.reshape(16, 8, BLOCK))
        both = jnp.concatenate(halves, axis=1).astype(BF16)
        start = pl.multiple_of(p * 16, 16)
        for b in range(16):
            turned_ref[b, pl.ds(start, 16), :] = both[b]
        return carry

    lax.fori_loop(0, 8, pair, 0, unroll=4)
    for b in range(16):
        out_ref[0, b * BLOCK : (b + 1) * BLOCK, :] = turned_ref[b].T


def spread_of(small):
    sources = small.shape[0]
    return pl.pallas_call(
        spread_body,
        grid=(sources, 8),
        in_specs=[
            pl.BlockSpec((1, 16, 256), lambda s, i: (s, i, 0)),
            pl.BlockSpec((1, 16, 256), lambda s, i: (s, i + 8, 0)),
        ],
        out_specs=pl.BlockSpec((1, 2048, 128), lambda s, i: (s, 0, i)),
        out_shape=jax.ShapeDtypeStruct((sources, 2048, 1024), BF16),
        scratch_shapes=[pltpu.VMEM((16, 128, BLOCK), BF16)],
        cost_estimate=pl.CostEstimate(
            flops=sources * 2**32, bytes_accessed=sources * 2**22, transcendentals=0
        ),
        name="spread",
    )(small, small)


def merge_body(place_ref, grad_ref, spread_ref, own_ref, send_ref):
    s = pl.program_id(0)

    @pl.when(s == 0)
    def _():
        own_ref[...] = jnp.zeros_like(own_ref)
        send_ref[...] = jnp.zeros_like(send_ref)

    grad = grad_ref[0].astype(BF16)

    def pair(p, carry):
        start = pl.multiple_of(p * 256, 256)
        part = jnp.dot(
            spread_ref[0, pl.ds(start, 256), :], grad, preferred_element_type=F32
        )
        for h in range(2):
            place = place_ref[s, 2 * p + h]

            @pl.when(place >= 0)
            def _():
                side, at = place >> 5, place & 31
                for y in range(4):
                    r = h * 128 + y * 32
                    own_ref[side, y, at] += part[r : r + 16]
                    send_ref[side, y, at] += part[r + 16 : r + 32]

        return carry

    lax.fori_loop(0, 8, pair, 0)


def merge(places, grads, spreads):
    sources, tokens, width = grads.shape
    dense = jax.ShapeDtypeStruct((2, 4, 32, 16, width), F32)
    block = pl.BlockSpec((2, 4, 32, 16, width), lambda s, c: (0, 0, 0, 0, 0))
    return pl.pallas_call(
        merge_body,
        grid_spec=pltpu.PrefetchScalarGridSpec(
            num_scalar_prefetch=1,
            grid=(sources,),
            in_specs=[
                pl.BlockSpec((1, tokens, width), lambda s, c: (s, 0, 0)),
                pl.BlockSpec((1, 2048, tokens), lambda s, c: (s, 0, 0)),
            ],
            out_specs=[block, block],
        ),
        out_shape=[dense, dense],
        cost_estimate=pl.CostEstimate(
            flops=sources * 2 * 2048 * tokens * width,
            bytes_accessed=sources * tokens * (4096 + 4 * width) + 2**22,
            transcendentals=0,
        ),
        name="merge",
    )(places, grads, spreads)


def adam_update(gradient, param, first_moment, second_moment):
    new_first = first_decay * first_moment + (1.0 - first_decay) * gradient
    new_second = second_decay * second_moment + (1.0 - second_decay) * gradient * gradient
    new_param = param - learning_rate * (new_first * first_debias) / (
        jnp.sqrt(new_second * second_debias) + adam_epsilon
    )
    return (new_param, new_first, new_second)


def flip(x, axis, bits):
    size = lax.axis_size(axis)
    return lax.ppermute(x, axis, [(i, i ^ bits) for i in range(size)])


def other_neighbour(x):
    return lax.ppermute(x, "gz", [(i, (((i + 1) ^ 1) - 1) % 16) for i in range(16)])


def to_chip(own, send):
    got = flip(send, "gy", 1)
    low = own[1, :, :16] + got[1, :, :16]
    high = own[1, :, 16:] + got[1, :, 16:]
    return own, got, low, high


def to_owners(own, got, low, high):
    width = own.shape[-1]
    near = [flip(low, "gz", 1), other_neighbour(high)]

    def kept(y):
        near_rows = jnp.concatenate([near[0][y], near[1][y]], axis=0)
        return own[0, y] + got[0, y] + near_rows

    rows = kept(0)
    for piece in [flip(kept(y), "gy", 2 * y) for y in (1, 3, 2)]:
        rows = rows + piece
    far = lax.all_to_all(
        rows,
        ("gx", "gz"),
        0,
        0,
        axis_index_groups=[
            [
                (2 * half + low) * 16 + 2 * u + i
                for half in range(2)
                for u in range(8)
                for low in range(2)
            ]
            for i in range(2)
        ],
        tiled=True,
    )
    far = jnp.sum(far.reshape(2, 8, 2, 16, width), axis=1)
    return far.reshape(4, 16, width)


def shards(
    output_grad, entries, weights, hot_blocks, block_counts, param, first_moment, second_moment
):
    gy = lax.axis_index("gy")
    gz = lax.axis_index("gz")
    listed = hot_blocks[0]
    slots = jnp.arange(16, dtype=jnp.int32)
    usable = (slots < block_counts[0]) & (listed >= 0)
    blocks = jnp.where(usable, listed, -1).astype(F32)

    code = (entries ^ (gy * 16)).astype(F32)
    small = jnp.concatenate(
        [
            code.reshape(128, 256),
            weights.astype(F32).reshape(128, 256),
            jnp.broadcast_to(jnp.pad(blocks, (0, 240))[None], (8, 256)),
        ],
        axis=0,
    )
    small = lax.all_to_all(
        jnp.broadcast_to(small[None], (4, 264, 256)), "gx", 0, 0, tiled=True
    )
    spreads = spread_of(small)
    blocks = small[:, 256, :16].astype(jnp.int32)
    bucket = blocks & 15
    column = blocks >> 4
    side = (bucket ^ gz) & 1
    places = side * 32 + (column >> 1) * 16 + (bucket >> 1) * 2 + (column & 1)
    places = jnp.where(blocks >= 0, places, -1)

    first, second = widen(output_grad)
    first = lax.all_to_all(first, "gx", 0, 0, tiled=True)
    second, spreads = lax.optimization_barrier((second, spreads))
    second = lax.all_to_all(second, "gx", 0, 0, tiled=True)
    first = merge(places, first, spreads)
    own, got, low, high = to_chip(*first)
    second, low, high = lax.optimization_barrier((second, low, high))
    second = merge(places, second, spreads)
    pieces = [to_owners(own, got, low, high), to_owners(*to_chip(*second))]
    gradient = jnp.stack(pieces, axis=1)
    gradient = jnp.moveaxis(gradient, 2, 0).reshape(param.shape)
    return adam_update(gradient, param, first_moment, second_moment)


def solution(mesh):
    placed = (
        P(("gx", "gy", "gz"), None),
        P(("gx", "gy", "gz"), None),
        P(("gx", "gy", "gz"), None),
        P(("gx", "gy", "gz"), None),
        P(("gx", "gy", "gz")),
        P("gx", "gz", "gy", None),
        P("gx", "gz", "gy", None),
        P("gx", "gz", "gy", None),
    )

    return jax.shard_map(
        shards,
        mesh=mesh,
        in_specs=placed,
        out_specs=(P("gx", "gz", "gy", None), P("gx", "gz", "gy", None), P("gx", "gz", "gy", None)),
        check_vma=False,
    )
```

time: 234 us -> 244 us (1.043)
  the two profiles are of different devices: /device:TPU:1 before, /device:TPU:16 now
where the time goes in v2:
time: 244 us; the launch traced here: 242 us
  waiting for transfers between devices  81.9 us (34%)
  starting transfers between devices  76.4 us (31%)
  Pallas kernels  64.6 us (26%)
  other arithmetic  9.79 us (4%)
  local copies, waits for them, and re-layouts  8.02 us (3%)
    pallas_call x2, Pallas kernels, merge(): pl.pallas_call(merge_body, grid_spec=pltpu.PrefetchScalarGridSpec(num_sca...  30.5 us
    pallas_call x1, Pallas kernels, spread_of(): pl.pallas_call(spread_body, grid=(sources, 8), in_specs=[pl.BlockSpec((1,...  29.9 us
    ppermute x10, starting transfers between devices, flip(): return lax.ppermute(x, axis, [(i, i ^ bits) for i in range(size)])  29.5 us
    all_to_all x1, waiting for transfers between devices, shards(): second = lax.all_to_all(second, 'gx', 0, 0, tiled=True)  25.3 us
    all_to_all x2, waiting for transfers between devices, to_owners(): lax.all_to_all(rows, ('gx', 'gz'), 0, 0, axis_index_groups=[[(2 * half +...  19.6 us
    all_to_all x2, starting transfers between devices, to_owners(): lax.all_to_all(rows, ('gx', 'gz'), 0, 0, axis_index_groups=[[(2 * half +...  18.9 us
    ppermute x2, waiting for transfers between devices, other_neighbour(): lax.ppermute(x, 'gz', [(i, ((i + 1 ^ 1) - 1) % 16) for i in range(16)])  18.4 us
    ppermute x2, starting transfers between devices, other_neighbour(): lax.ppermute(x, 'gz', [(i, ((i + 1 ^ 1) - 1) % 16) for i in range(16)])  15.3 us
  transfers between devices with their start and end apart: 17, of which 8 were waited for; matrix products, arithmetic and copies ran while one was open for 3% of the time, Pallas kernels for 14%

profile of v2, /device:TPU:16, one launch (start us, length us, event | category | flops | bytes accessed | tf_op | source)
XLA Modules:
  0.0 242.4 jit_solution(15041162805042668259)
XLA Ops:
  0.6 0.9 xor_convert_fusion
  1.6 0.2 copy.16
  1.8 0.2 reshape.95
  2.0 1.0 copy.17
  2.9 0.2 reshape.102
  3.8 1.1 broadcast_in_dim.22
  4.9 4.3 %all-to-all-start = ((f32[4,264,256]{2,1,0:T(8,128)}), f32[4,264,256]{2,1,0:T(8,128)S(1)}, u32[]{:S(2)}, u32[]{:S(2)}) async-start(f32[4,264,256]{2,1,0:T(8,128)} %broadcast_in_dim.22), calls=%async_computation | async-start | bytes 2162688 | tf_op jit(solution)/shard_map/all_to_all | solution.py:220
  9.2 4.2 %widen.1 = (f32[4,1024,128]{2,1,0:T(8,128)}, f32[4,1024,128]{2,1,0:T(8,128)}) custom-call(bf16[1024,1024]{1,0:T(8,128)(2,1)} %grad_ref.1), custom_call_target="tpu_custom_call" | custom-call | flops 8388608 | bytes 6291456 | tf_op jit(solution)/shard_map/widen/pallas_call | solution.py:31
  13.4 11.2 %all-to-all-done.code_ref.wgt_ref = f32[4,264,256]{2,1,0:T(8,128)S(1)} async-done(((f32[4,264,256]{2,1,0:T(8,128)}), f32[4,264,256]{2,1,0:T(8,128)S(1)}, u32[]{:S(2)}, u32[]{:S(2)}) %all-to-all-start) | async-done | bytes 1081376 | tf_op jit(solution)/shard_map/all_to_all | solution.py:220
  24.6 1.0 copy-done.6
  25.7 3.6 %all-to-all-start.1 = ((f32[4,1024,128]{2,1,0:T(8,128)}), f32[4,1024,128]{2,1,0:T(8,128)S(1)}, u32[]{:S(2)}, u32[]{:S(2)}) async-start(f32[4,1024,128]{2,1,0:T(8,128)} %get-tuple-element.14), calls=%async_computation.1 | async-start | bytes 4194304 | tf_op jit(solution)/shard_map/all_to_all | solution.py:232
  29.3 29.9 %spread.1.spread_ref = bf16[4,2048,1024]{2,1,0:T(8,128)(2,1)} custom-call(f32[4,264,256]{2,1,0:T(8,128)} %copy-done.6, f32[4,264,256]{2,1,0:T(8,128)} %copy-done.6), custom_call_target="tpu_custom_call" | custom-call | flops 17179869184 | bytes 16777216 | tf_op jit(solution)/shard_map/spread/pallas_call | solution.py:72
  59.2 1.3 compare_select_fusion
  60.5 1.4 copy-done.1
  61.9 15.2 %merge.2 = (f32[2,4,32,16,128]{4,3,2,1,0:T(8,128)}, f32[2,4,32,16,128]{4,3,2,1,0:T(8,128)}) custom-call(s32[4,16]{1,0:T(4,128)} %bitcast.101, f32[4,1024,128]{2,1,0:T(8,128)} %copy-done.1, bf16[4,2048,1024]{2,1,0:T(8,128)(2,1)} %spread.1.spread_ref), custom_call_target="tpu_custom_call" | custom-call | flops 2147483648 | bytes 23068672 | tf_op jit(solution)/shard_map/merge/pallas_call | solution.py:124
  77.1 1.9 collective-permute-start
  79.0 4.8 %all-to-all-start.2 = ((f32[4,1024,128]{2,1,0:T(8,128)}), f32[4,1024,128]{2,1,0:T(8,128)S(1)}, u32[]{:S(2)}, u32[]{:S(2)}) async-start(f32[4,1024,128]{2,1,0:T(8,128)} %get-tuple-element.19), calls=%async_computation.2 | async-start | bytes 4194304 | tf_op jit(solution)/shard_map/all_to_all | solution.py:234
  83.8 1.7 fusion.2
  85.5 25.3 %all-to-all-done.2.grad_ref = f32[4,1024,128]{2,1,0:T(8,128)S(1)} async-done(((f32[4,1024,128]{2,1,0:T(8,128)}), f32[4,1024,128]{2,1,0:T(8,128)S(1)}, u32[]{:S(2)}, u32[]{:S(2)}) %all-to-all-start.2) | async-done | bytes 2097184 | tf_op jit(solution)/shard_map/all_to_all | solution.py:234
  110.8 1.4 copy-done
  112.2 15.3 %merge.3 = (f32[2,4,32,16,128]{4,3,2,1,0:T(8,128)}, f32[2,4,32,16,128]{4,3,2,1,0:T(8,128)}) custom-call(s32[4,16]{1,0:T(4,128)} %bitcast.102, f32[4,1024,128]{2,1,0:T(8,128)} %copy-done, bf16[4,2048,1024]{2,1,0:T(8,128)(2,1)} %spread.1.spread_ref), custom_call_target="tpu_custom_call" | custom-call | flops 2147483648 | bytes 23068672 | tf_op jit(solution)/shard_map/merge/pallas_call | solution.py:124
  127.4 2.0 collective-permute-start.6
  129.5 3.9 %collective-permute-start.1 = (f32[4,16,16,128]{3,2,1,0:T(8,128)S(1)}, f32[4,16,16,128]{3,2,1,0:T(8,128)S(1)}, u32[]{:S(2)}, u32[]{:S(2)}) collective-permute-start(f32[4,16,16,128]{3,2,1,0:T(8,128)S(1)} %get-tuple-element.20), channel_id=1, source_target_pairs={{0,1},{1,0},{2,3},{3,2},{4,5},{5,4},{6,7},{7,6},{8,9},{9,8},{10,11... | collective-permute-start | bytes 1572872 | tf_op jit(solution)/shard_map/ppermute | solution.py:156
  133.4 10.4 %collective-permute-start.2 = (f32[4,16,16,128]{3,2,1,0:T(8,128)S(1)}, f32[4,16,16,128]{3,2,1,0:T(8,128)S(1)}, u32[]{:S(2)}, u32[]{:S(2)}) collective-permute-start(f32[4,16,16,128]{3,2,1,0:T(8,128)S(1)} %get-tuple-element.21), channel_id=1, source_target_pairs={{0,15},{1,2},{2,1},{3,4},{4,3},{5,6},{6,5},{7,8},{8,7},{9,10},{10,... | collective-permute-start | bytes 1572872 | tf_op jit(solution)/shard_map/ppermute | solution.py:160
  143.8 2.1 collective-permute-done.1
  146.0 10.1 %collective-permute-done.2 = f32[4,16,16,128]{3,2,1,0:T(8,128)S(1)} collective-permute-done((f32[4,16,16,128]{3,2,1,0:T(8,128)S(1)}, f32[4,16,16,128]{3,2,1,0:T(8,128)S(1)}, u32[]{:S(2)}, u32[]{:S(2)}) %collective-permute-start.2) | collective-permute-done | bytes 524320 | tf_op jit(solution)/shard_map/ppermute | solution.py:160
  156.1 1.3 fusion.20
  157.4 3.2 %collective-permute-start.3 = (f32[32,16,128]{2,1,0:T(8,128)S(1)}, f32[32,16,128]{2,1,0:T(8,128)S(1)}, u32[]{:S(2)}, u32[]{:S(2)}) collective-permute-start(f32[32,16,128]{2,1,0:T(8,128)S(1)} %get-tuple-element.28), channel_id=1, source_target_pairs={{0,32},{16,48},{32,0},{48,16},{64,96},{80,112},{96,64},{112,80},{1... | collective-permute-start | bytes 786440 | tf_op jit(solution)/shard_map/ppermute | solution.py:156
  160.6 1.9 collective-permute-start.4
  162.6 4.7 %collective-permute-start.5 = (f32[32,16,128]{2,1,0:T(8,128)S(1)}, f32[32,16,128]{2,1,0:T(8,128)S(1)}, u32[]{:S(2)}, u32[]{:S(2)}) collective-permute-start(f32[32,16,128]{2,1,0:T(8,128)S(1)} %get-tuple-element.29), channel_id=1, source_target_pairs={{0,64},{16,80},{32,96},{48,112},{64,0},{80,16},{96,32},{112,48},{1... | collective-permute-start | bytes 786440 | tf_op jit(solution)/shard_map/ppermute | solution.py:156
  167.3 1.4 copy-done.3
  168.6 1.1 fusion.1
  169.8 1.9 collective-permute-start.7
  171.7 4.9 %collective-permute-start.8 = (f32[4,16,16,128]{3,2,1,0:T(8,128)}, f32[4,16,16,128]{3,2,1,0:T(8,128)S(1)}, u32[]{:S(2)}, u32[]{:S(2)}) collective-permute-start(f32[4,16,16,128]{3,2,1,0:T(8,128)} %get-tuple-element.35), channel_id=1, source_target_pairs={{0,15},{1,2},{2,1},{3,4},{4,3},{5,6},{6,5},{7,8},{8,7},{9,10},{10,... | collective-permute-start | bytes 1572872 | tf_op jit(solution)/shard_map/ppermute | solution.py:160
  176.6 1.8 fusion.25
  178.3 8.4 %all-to-all-start.3 = ((f32[32,16,128]{2,1,0:T(8,128)}), f32[32,16,128]{2,1,0:T(8,128)S(1)}, u32[]{:S(2)}, u32[]{:S(2)}) async-start(f32[32,16,128]{2,1,0:T(8,128)} %fusion.25), calls=%async_computation.3 | async-start | bytes 524288 | tf_op jit(solution)/shard_map/all_to_all | solution.py:181
  186.8 8.3 %collective-permute-done.8 = f32[4,16,16,128]{3,2,1,0:T(8,128)S(1)} collective-permute-done((f32[4,16,16,128]{3,2,1,0:T(8,128)}, f32[4,16,16,128]{3,2,1,0:T(8,128)S(1)}, u32[]{:S(2)}, u32[]{:S(2)}) %collective-permute-start.8) | collective-permute-done | bytes 524320 | tf_op jit(solution)/shard_map/ppermute | solution.py:160
  195.2 0.2 fusion.9
  195.4 3.0 %collective-permute-start.10 = (f32[32,16,128]{2,1,0:T(8,128)S(1)}, f32[32,16,128]{2,1,0:T(8,128)S(1)}, u32[]{:S(2)}, u32[]{:S(2)}) collective-permute-start(f32[32,16,128]{2,1,0:T(8,128)S(1)} %get-tuple-element.33), channel_id=1, source_target_pairs={{0,96},{16,112},{32,64},{48,80},{64,32},{80,48},{96,0},{112,16},{1... | collective-permute-start | bytes 786440 | tf_op jit(solution)/shard_map/ppermute | solution.py:156
  198.4 3.5 %collective-permute-start.11 = (f32[32,16,128]{2,1,0:T(8,128)S(1)}, f32[32,16,128]{2,1,0:T(8,128)S(1)}, u32[]{:S(2)}, u32[]{:S(2)}) collective-permute-start(f32[32,16,128]{2,1,0:T(8,128)S(1)} %get-tuple-element.32), channel_id=1, source_target_pairs={{0,64},{16,80},{32,96},{48,112},{64,0},{80,16},{96,32},{112,48},{1... | collective-permute-start | bytes 786440 | tf_op jit(solution)/shard_map/ppermute | solution.py:156
  201.8 3.5 %collective-permute-start.9 = (f32[32,16,128]{2,1,0:T(8,128)S(1)}, f32[32,16,128]{2,1,0:T(8,128)S(1)}, u32[]{:S(2)}, u32[]{:S(2)}) collective-permute-start(f32[32,16,128]{2,1,0:T(8,128)S(1)} %get-tuple-element.31), channel_id=1, source_target_pairs={{0,32},{16,48},{32,0},{48,16},{64,96},{80,112},{96,64},{112,80},{1... | collective-permute-start | bytes 786440 | tf_op jit(solution)/shard_map/ppermute | solution.py:156
  205.4 2.8 %collective-permute-done.11 = f32[32,16,128]{2,1,0:T(8,128)S(1)} collective-permute-done((f32[32,16,128]{2,1,0:T(8,128)S(1)}, f32[32,16,128]{2,1,0:T(8,128)S(1)}, u32[]{:S(2)}, u32[]{:S(2)}) %collective-permute-start.11) | collective-permute-done | bytes 262176 | tf_op jit(solution)/shard_map/ppermute | solution.py:156
  208.2 2.4 %collective-permute-done.9 = f32[32,16,128]{2,1,0:T(8,128)S(1)} collective-permute-done((f32[32,16,128]{2,1,0:T(8,128)S(1)}, f32[32,16,128]{2,1,0:T(8,128)S(1)}, u32[]{:S(2)}, u32[]{:S(2)}) %collective-permute-start.9) | collective-permute-done | bytes 262176 | tf_op jit(solution)/shard_map/ppermute | solution.py:156
  210.6 0.8 fusion.14
  211.4 10.5 %all-to-all-start.4 = ((f32[32,16,128]{2,1,0:T(8,128)}), f32[32,16,128]{2,1,0:T(8,128)S(1)}, u32[]{:S(2)}, u32[]{:S(2)}) async-start(f32[32,16,128]{2,1,0:T(8,128)} %fusion.14), calls=%async_computation.4 | async-start | bytes 524288 | tf_op jit(solution)/shard_map/all_to_all | solution.py:181
  221.9 19.6 %all-to-all-done.4 = f32[32,16,128]{2,1,0:T(8,128)S(1)} async-done(((f32[32,16,128]{2,1,0:T(8,128)}), f32[32,16,128]{2,1,0:T(8,128)S(1)}, u32[]{:S(2)}, u32[]{:S(2)}) %all-to-all-start.4) | async-done | bytes 262176 | tf_op jit(solution)/shard_map/all_to_all | solution.py:181
  241.7 0.1 reshape.100
  241.8 0.7 divide_subtract_fusion
  (39 shorter events, 0.3 us)
Async XLA Ops:
  0.6 3.1 %copy-start.10 = (s32[1,16]{1,0:T(1,128)S(1)}, s32[1,16]{1,0:T(1,128)}, u32[]{:S(2)}) copy-start(s32[1,16]{1,0:T(1,128)} %param.11) | copy-start | bytes 196
  4.9 19.7 %all-to-all-start = ((f32[4,264,256]{2,1,0:T(8,128)}), f32[4,264,256]{2,1,0:T(8,128)S(1)}, u32[]{:S(2)}, u32[]{:S(2)}) async-start(f32[4,264,256]{2,1,0:T(8,128)} %broadcast_in_dim.22), calls=%async_computation | async-start | bytes 2162688 | tf_op jit(solution)/shard_map/all_to_all | solution.py:220
  24.6 1.0 copy-start.6
  25.7 34.8 %all-to-all-start.1 = ((f32[4,1024,128]{2,1,0:T(8,128)}), f32[4,1024,128]{2,1,0:T(8,128)S(1)}, u32[]{:S(2)}, u32[]{:S(2)}) async-start(f32[4,1024,128]{2,1,0:T(8,128)} %get-tuple-element.14), calls=%async_computation.1 | async-start | bytes 4194304 | tf_op jit(solution)/shard_map/all_to_all | solution.py:232
  60.5 1.4 copy-start.1
  77.1 6.7 %collective-permute-start = (f32[2,4,32,16,128]{4,3,2,1,0:T(8,128)}, f32[2,4,32,16,128]{4,3,2,1,0:T(8,128)}, u32[]{:S(2)}, u32[]{:S(2)}) collective-permute-start(f32[2,4,32,16,128]{4,3,2,1,0:T(8,128)} %get-tuple-element.18), channel_id=1, source_target_pairs={{0,16},{16,0},{32,48},{48,32},{64,80},{80,64},{96,112},{112,96},{1... | collective-permute-start | bytes 6291464 | tf_op jit(solution)/shard_map/ppermute | solution.py:156
  79.0 31.8 %all-to-all-start.2 = ((f32[4,1024,128]{2,1,0:T(8,128)}), f32[4,1024,128]{2,1,0:T(8,128)S(1)}, u32[]{:S(2)}, u32[]{:S(2)}) async-start(f32[4,1024,128]{2,1,0:T(8,128)} %get-tuple-element.19), calls=%async_computation.2 | async-start | bytes 4194304 | tf_op jit(solution)/shard_map/all_to_all | solution.py:234
  110.8 1.4 copy-start
  127.4 28.7 %copy-start.5 = (f32[2,4,32,16,128]{4,3,2,1,0:T(8,128)S(1)}, f32[2,4,32,16,128]{4,3,2,1,0:T(8,128)}, u32[]{:S(2)}) copy-start(f32[2,4,32,16,128]{4,3,2,1,0:T(8,128)} %get-tuple-element.17) | copy-start | bytes 6291460
  127.4 39.8 %collective-permute-start.6 = (f32[2,4,32,16,128]{4,3,2,1,0:T(8,128)}, f32[2,4,32,16,128]{4,3,2,1,0:T(8,128)S(1)}, u32[]{:S(2)}, u32[]{:S(2)}) collective-permute-start(f32[2,4,32,16,128]{4,3,2,1,0:T(8,128)} %get-tuple-element.24), channel_id=1, source_target_pairs={{0,16},{16,0},{32,48},{48,32},{64,80},{80,64},{96,112},{112,96},{1... | collective-permute-start | bytes 6291464 | tf_op jit(solution)/shard_map/ppermute | solution.py:156
  129.5 16.5 %collective-permute-start.1 = (f32[4,16,16,128]{3,2,1,0:T(8,128)S(1)}, f32[4,16,16,128]{3,2,1,0:T(8,128)S(1)}, u32[]{:S(2)}, u32[]{:S(2)}) collective-permute-start(f32[4,16,16,128]{3,2,1,0:T(8,128)S(1)} %get-tuple-element.20), channel_id=1, source_target_pairs={{0,1},{1,0},{2,3},{3,2},{4,5},{5,4},{6,7},{7,6},{8,9},{9,8},{10,11... | collective-permute-start | bytes 1572872 | tf_op jit(solution)/shard_map/ppermute | solution.py:156
  133.4 22.7 %collective-permute-start.2 = (f32[4,16,16,128]{3,2,1,0:T(8,128)S(1)}, f32[4,16,16,128]{3,2,1,0:T(8,128)S(1)}, u32[]{:S(2)}, u32[]{:S(2)}) collective-permute-start(f32[4,16,16,128]{3,2,1,0:T(8,128)S(1)} %get-tuple-element.21), channel_id=1, source_target_pairs={{0,15},{1,2},{2,1},{3,4},{4,3},{5,6},{6,5},{7,8},{8,7},{9,10},{10,... | collective-permute-start | bytes 1572872 | tf_op jit(solution)/shard_map/ppermute | solution.py:160
  146.0 22.7 %copy-start.2 = (f32[2,4,32,16,128]{4,3,2,1,0:T(8,128)S(1)}, f32[2,4,32,16,128]{4,3,2,1,0:T(8,128)}, u32[]{:S(2)}) copy-start(f32[2,4,32,16,128]{4,3,2,1,0:T(8,128)} %get-tuple-element.23) | copy-start | bytes 6291460
  157.4 19.1 %collective-permute-start.3 = (f32[32,16,128]{2,1,0:T(8,128)S(1)}, f32[32,16,128]{2,1,0:T(8,128)S(1)}, u32[]{:S(2)}, u32[]{:S(2)}) collective-permute-start(f32[32,16,128]{2,1,0:T(8,128)S(1)} %get-tuple-element.28), channel_id=1, source_target_pairs={{0,32},{16,48},{32,0},{48,16},{64,96},{80,112},{96,64},{112,80},{1... | collective-permute-start | bytes 786440 | tf_op jit(solution)/shard_map/ppermute | solution.py:156
  160.6 15.9 %collective-permute-start.4 = (f32[32,16,128]{2,1,0:T(8,128)S(1)}, f32[32,16,128]{2,1,0:T(8,128)S(1)}, u32[]{:S(2)}, u32[]{:S(2)}) collective-permute-start(f32[32,16,128]{2,1,0:T(8,128)S(1)} %get-tuple-element.30), channel_id=1, source_target_pairs={{0,96},{16,112},{32,64},{48,80},{64,32},{80,48},{96,0},{112,16},{1... | collective-permute-start | bytes 786440 | tf_op jit(solution)/shard_map/ppermute | solution.py:156
  162.6 14.0 %collective-permute-start.5 = (f32[32,16,128]{2,1,0:T(8,128)S(1)}, f32[32,16,128]{2,1,0:T(8,128)S(1)}, u32[]{:S(2)}, u32[]{:S(2)}) collective-permute-start(f32[32,16,128]{2,1,0:T(8,128)S(1)} %get-tuple-element.29), channel_id=1, source_target_pairs={{0,64},{16,80},{32,96},{48,112},{64,0},{80,16},{96,32},{112,48},{1... | collective-permute-start | bytes 786440 | tf_op jit(solution)/shard_map/ppermute | solution.py:156
  167.3 1.4 copy-start.3
  169.8 17.0 %collective-permute-start.7 = (f32[4,16,16,128]{3,2,1,0:T(8,128)}, f32[4,16,16,128]{3,2,1,0:T(8,128)S(1)}, u32[]{:S(2)}, u32[]{:S(2)}) collective-permute-start(f32[4,16,16,128]{3,2,1,0:T(8,128)} %get-tuple-element.34), channel_id=1, source_target_pairs={{0,1},{1,0},{2,3},{3,2},{4,5},{5,4},{6,7},{7,6},{8,9},{9,8},{10,11... | collective-permute-start | bytes 1572872 | tf_op jit(solution)/shard_map/ppermute | solution.py:156
  171.7 23.5 %collective-permute-start.8 = (f32[4,16,16,128]{3,2,1,0:T(8,128)}, f32[4,16,16,128]{3,2,1,0:T(8,128)S(1)}, u32[]{:S(2)}, u32[]{:S(2)}) collective-permute-start(f32[4,16,16,128]{3,2,1,0:T(8,128)} %get-tuple-element.35), channel_id=1, source_target_pairs={{0,15},{1,2},{2,1},{3,4},{4,3},{5,6},{6,5},{7,8},{8,7},{9,10},{10,... | collective-permute-start | bytes 1572872 | tf_op jit(solution)/shard_map/ppermute | solution.py:160
  178.3 33.1 %all-to-all-start.3 = ((f32[32,16,128]{2,1,0:T(8,128)}), f32[32,16,128]{2,1,0:T(8,128)S(1)}, u32[]{:S(2)}, u32[]{:S(2)}) async-start(f32[32,16,128]{2,1,0:T(8,128)} %fusion.25), calls=%async_computation.3 | async-start | bytes 524288 | tf_op jit(solution)/shard_map/all_to_all | solution.py:181
  186.8 8.4 %copy-start.4 = (f32[2,4,32,16,128]{4,3,2,1,0:T(8,128)S(1)}, f32[2,4,32,16,128]{4,3,2,1,0:T(8,128)}, u32[]{:S(2)}) copy-start(f32[2,4,32,16,128]{4,3,2,1,0:T(8,128)} %copy-done.3) | copy-start | bytes 6291460
  195.4 46.4 %copy-start.7 = (f32[1,1,16,1024]{3,2,1,0:T(8,128)S(1)}, f32[1,1,16,1024]{3,2,1,0:T(8,128)}, u32[]{:S(2)}) copy-start(f32[1,1,16,1024]{3,2,1,0:T(8,128)} %param.13) | copy-start | bytes 196612
  195.4 46.4 %copy-start.8 = (f32[1,1,16,1024]{3,2,1,0:T(8,128)S(1)}, f32[1,1,16,1024]{3,2,1,0:T(8,128)}, u32[]{:S(2)}) copy-start(f32[1,1,16,1024]{3,2,1,0:T(8,128)} %param.14) | copy-start | bytes 196612
  195.4 46.4 %copy-start.9 = (f32[1,1,16,1024]{3,2,1,0:T(8,128)S(1)}, f32[1,1,16,1024]{3,2,1,0:T(8,128)}, u32[]{:S(2)}) copy-start(f32[1,1,16,1024]{3,2,1,0:T(8,128)} %param.15) | copy-start | bytes 196612
  195.4 10.0 %collective-permute-start.10 = (f32[32,16,128]{2,1,0:T(8,128)S(1)}, f32[32,16,128]{2,1,0:T(8,128)S(1)}, u32[]{:S(2)}, u32[]{:S(2)}) collective-permute-start(f32[32,16,128]{2,1,0:T(8,128)S(1)} %get-tuple-element.33), channel_id=1, source_target_pairs={{0,96},{16,112},{32,64},{48,80},{64,32},{80,48},{96,0},{112,16},{1... | collective-permute-start | bytes 786440 | tf_op jit(solution)/shard_map/ppermute | solution.py:156
  198.4 9.8 %collective-permute-start.11 = (f32[32,16,128]{2,1,0:T(8,128)S(1)}, f32[32,16,128]{2,1,0:T(8,128)S(1)}, u32[]{:S(2)}, u32[]{:S(2)}) collective-permute-start(f32[32,16,128]{2,1,0:T(8,128)S(1)} %get-tuple-element.32), channel_id=1, source_target_pairs={{0,64},{16,80},{32,96},{48,112},{64,0},{80,16},{96,32},{112,48},{1... | collective-permute-start | bytes 786440 | tf_op jit(solution)/shard_map/ppermute | solution.py:156
  201.8 8.7 %collective-permute-start.9 = (f32[32,16,128]{2,1,0:T(8,128)S(1)}, f32[32,16,128]{2,1,0:T(8,128)S(1)}, u32[]{:S(2)}, u32[]{:S(2)}) collective-permute-start(f32[32,16,128]{2,1,0:T(8,128)S(1)} %get-tuple-element.31), channel_id=1, source_target_pairs={{0,32},{16,48},{32,0},{48,16},{64,96},{80,112},{96,64},{112,80},{1... | collective-permute-start | bytes 786440 | tf_op jit(solution)/shard_map/ppermute | solution.py:156
  211.4 30.2 %all-to-all-start.4 = ((f32[32,16,128]{2,1,0:T(8,128)}), f32[32,16,128]{2,1,0:T(8,128)S(1)}, u32[]{:S(2)}, u32[]{:S(2)}) async-start(f32[32,16,128]{2,1,0:T(8,128)} %fusion.14), calls=%async_computation.4 | async-start | bytes 524288 | tf_op jit(solution)/shard_map/all_to_all | solution.py:181
